TPU v7x, 32 devices: a whole 2x2x4 slice. The times are simulated.
32 devices in a mesh: groups: 2 (over x), row: 16 (over z, y, core).
Axes of the slice: x: 2, y: 2, z: 4, core: 2. Of those that a mesh axis runs over, the one named last changes fastest.
Arguments:
- design_matrix: bfloat16 [1024, 65536], P('groups', 'row'), parts along dimension 0, may hold values from -0.0546875 to 0.0546875
- targets: float32 [1024, 128], P(('groups', 'row')), parts along dimension 0, may hold values from -24 to 24
- linear: float32 [131072, 128], P(('groups', 'row')), parts along dimension 0, may hold values from -24 to 24
- diagonal: float32 [131072], P(('groups', 'row')), parts along dimension 0, may hold values from 0.1 to 2
- lower_code: int32 [131072, 128], P(('groups', 'row')), parts along dimension 0, may hold values from -192 to -17
- upper_code: int32 [131072, 128], P(('groups', 'row')), parts along dimension 0, may hold values from 16 to 191
Outputs:
- box_iterate: float32 [131072, 128], P(('groups', 'row')), parts along dimension 0
- scaled_dual: float32 [131072, 128], P(('groups', 'row')), parts along dimension 0
There are 2 independent parts, one for each index of `groups`. A program takes and returns all parts, laid end to end along the dimension named above; each array names one. Nothing has to cross between parts.
All inputs are finite; a program needn't handle non-finite values.
Results may differ from a plain program's by a relative error of at most 0.00033.
Values may be sent and summed in bfloat16 or wider, within the bound.
A program may use at most 128 MiB of HBM per device.

v0:
```python
import functools

import jax
import jax.numpy as jnp
from jax import lax
from jax.experimental import pallas as pl
from jax.experimental.pallas import tpu as pltpu
from jax.sharding import PartitionSpec as P

ITERS = 4
TERM = jnp.float32

rho_plus_lip = 7.0


def solve_small(matrix, rhs):
    count = len(rhs)
    table = [list(line) for line in matrix]
    right = list(rhs)
    for p in range(count):
        for i in range(p + 1, count):
            factor = table[i][p] / table[p][p]
            for j in range(p, count):
                table[i][j] = table[i][j] - factor * table[p][j]
            right[i] = right[i] - factor * right[p]
    result = [None] * count
    for i in reversed(range(count)):
        total = right[i]
        for j in range(i + 1, count):
            total = total - table[i][j] * result[j]
        result[i] = total / table[i][i]
    return result


def mix_weights(gram):
    count = len(gram)
    trace = gram[0][0]
    for i in range(1, count):
        trace = trace + gram[i][i]
    shift = 0.01 * trace / count + 1e-06
    matrix = [[gram[i][j] + (shift if i == j else 0.0) for j in range(count)] for i in range(count)]
    solved = solve_small(matrix, [jnp.ones_like(trace)] * count)
    total = solved[0]
    for i in range(1, count):
        total = total + solved[i]
    return [item / total for item in solved]


def greet(n, me):
    barrier = pltpu.get_barrier_semaphore()
    for d in range(1, n):
        pl.semaphore_signal(
            barrier,
            inc=1,
            device_id={"row": lax.rem(me + d, n)},
            device_id_type=pl.DeviceIdType.MESH,
        )
    pl.semaphore_wait(barrier, n - 1)


def send(src, dst, send_sem, recv_sem, peer):
    copy = pltpu.make_async_remote_copy(
        src_ref=src,
        dst_ref=dst,
        send_sem=send_sem,
        recv_sem=recv_sem,
        device_id={"row": peer},
        device_id_type=pl.DeviceIdType.MESH,
    )
    copy.start()
    return copy


def spread(n, me, mine, whole, send_sem, recv_sem):
    copies = []
    for d in range(1, n):
        copies.append(
            send(mine, whole.at[me], send_sem.at[d], recv_sem.at[d], lax.rem(me + d, n))
        )
    whole[me] = mine[...]
    for copy in copies:
        copy.wait()


def chunks(local, size, body):
    def step(i, carry):
        body(pl.ds(pl.multiple_of(i * size, size), size))
        return carry

    lax.fori_loop(0, local // size, step, 0)


def column_sum(x):
    return jnp.sum(x, axis=0, keepdims=True)


def clip_codes(x, lo_ref, hi_ref, at):
    lower = lo_ref[at, :].astype(jnp.float32) * (1.0 / 64.0)
    upper = hi_ref[at, :].astype(jnp.float32) * (1.0 / 64.0)
    return jnp.minimum(jnp.maximum(x, lower), upper)


def whole_kernel(
    n,
    size,
    a_ref,
    targets_ref,
    lin_ref,
    diag_ref,
    lo_ref,
    hi_ref,
    z_ref,
    u_ref,
    mapped,
    changes,
    acc,
    terms,
    slots,
    mine,
    misfits,
    part,
    parts,
    grams,
    alpha_ref,
    send_a,
    recv_a,
    send_b,
    recv_b,
    send_c,
    recv_c,
):
    me = lax.axis_index("row")
    local = lin_ref.shape[0]
    k = a_ref.shape[0]

    def gradient_of(at):
        return lax.dot_general(
            a_ref[:, at],
            misfits[...].reshape(k, -1),
            (((0,), (0,)), ((), ())),
            preferred_element_type=jnp.float32,
        )

    def add_product(at, point):
        acc[...] += jnp.dot(
            a_ref[:, at], point.astype(jnp.bfloat16), preferred_element_type=jnp.float32
        )

    mine[...] = (0.0 - targets_ref[...]).astype(jnp.bfloat16)
    greet(n, me)
    spread(n, me, mine, misfits, send_b, recv_b)
    acc[...] = jnp.zeros_like(acc)
    part[...] = jnp.zeros_like(part)

    def start(at):
        gradient = gradient_of(at) + lin_ref[at, :]
        moved = 0.0 - (1.0 / (rho_plus_lip + diag_ref[at, :])) * gradient
        boxed = clip_codes(moved, lo_ref, hi_ref, at)
        scaled = moved - boxed
        mapped[0, 0, at, :] = boxed
        mapped[0, 1, at, :] = scaled
        part[7:8, :] += column_sum(boxed * boxed + scaled * scaled)
        add_product(at, boxed - scaled)

    chunks(local, size, start)

    for iteration in range(1, ITERS):
        count = iteration + 1
        last = iteration == ITERS - 1
        terms[...] = acc[...].reshape(terms.shape).astype(terms.dtype)
        copies = []
        for d in range(1, n):
            peer = lax.rem(me + d, n)
            copies.append(
                send(terms.at[peer], slots.at[d - 1], send_a.at[d], recv_a.at[d], peer)
            )
        total = terms[me].astype(jnp.float32)
        for d in range(1, n):
            copies[d - 1].wait_recv()
            total = total + slots[d - 1].astype(jnp.float32)
        mine[...] = (total - targets_ref[...]).astype(jnp.bfloat16)
        spread(n, me, mine, misfits, send_b, recv_b)
        for copy in copies:
            copy.wait_send()
        if iteration > 1:
            part[...] = jnp.zeros_like(part)

        def advance(at):
            if iteration == 1:
                z, u = mapped[0, 0, at, :], mapped[0, 1, at, :]
            else:
                z, u = z_ref[at, :], u_ref[at, :]
            point = z - u
            diagonal = diag_ref[at, :]
            gradient = gradient_of(at) + diagonal * point + lin_ref[at, :]
            moved = point - (1.0 / (rho_plus_lip + diagonal)) * gradient
            boxed = clip_codes(moved + u, lo_ref, hi_ref, at)
            scaled = u + moved - boxed
            mapped[iteration, 0, at, :] = boxed
            mapped[iteration, 1, at, :] = scaled
            cz, cu = boxed - z, scaled - u
            if not last:
                changes[iteration - 1, 0, at, :] = cz
                changes[iteration - 1, 1, at, :] = cu
            part[0:1, :] += column_sum(cz * mapped[0, 0, at, :] + cu * mapped[0, 1, at, :])
            for i in range(1, iteration):
                part[i:i + 1, :] += column_sum(
                    cz * changes[i - 1, 0, at, :] + cu * changes[i - 1, 1, at, :]
                )
            part[iteration:count, :] += column_sum(cz * cz + cu * cu)

        chunks(local, size, advance)

        spread(n, me, part, parts, send_c, recv_c)
        whole = parts[0]
        for i in range(1, n):
            whole = whole + parts[i]
        grams[iteration - 1] = whole

        gram = [[None] * count for _ in range(count)]
        gram[0][0] = grams[0, 7:8, :]
        for i in range(1, count):
            for j in range(i + 1):
                gram[i][j] = gram[j][i] = grams[i - 1, j:j + 1, :]
        for i, row in enumerate(mix_weights(gram)):
            alpha_ref[i:i + 1, :] = row
        acc[...] = jnp.zeros_like(acc)

        def mix(at):
            z = alpha_ref[0:1, :] * mapped[0, 0, at, :]
            u = alpha_ref[0:1, :] * mapped[0, 1, at, :]
            for i in range(1, count):
                z = z + alpha_ref[i:i + 1, :] * mapped[i, 0, at, :]
                u = u + alpha_ref[i:i + 1, :] * mapped[i, 1, at, :]
            z = clip_codes(z, lo_ref, hi_ref, at)
            z_ref[at, :] = z
            u_ref[at, :] = u
            if not last:
                add_product(at, z - u)

        chunks(local, size, mix)


def per_device(n, design_matrix, targets, linear, diagonal, lower_code, upper_code):
    k = design_matrix.shape[0]
    local, s = linear.shape
    kr = k // n
    big = jax.ShapeDtypeStruct((local, s), jnp.float32)
    vmem = pl.BlockSpec(memory_space=pltpu.VMEM)
    dma = pltpu.SemaphoreType.DMA((n,))
    return pl.pallas_call(
        functools.partial(whole_kernel, n, min(512, local)),
        in_specs=[vmem] * 6,
        out_specs=[vmem] * 2,
        out_shape=[big, big],
        scratch_shapes=[
            pltpu.VMEM((ITERS, 2, local, s), jnp.float32),
            pltpu.VMEM((ITERS - 2, 2, local, s), jnp.float32),
            pltpu.VMEM((k, s), jnp.float32),
            pltpu.VMEM((n, kr, s), TERM),
            pltpu.VMEM((n - 1, kr, s), TERM),
            pltpu.VMEM((kr, s), jnp.bfloat16),
            pltpu.VMEM((n, kr, s), jnp.bfloat16),
            pltpu.VMEM((8, s), jnp.float32),
            pltpu.VMEM((n, 8, s), jnp.float32),
            pltpu.VMEM((ITERS - 1, 8, s), jnp.float32),
            pltpu.VMEM((8, s), jnp.float32),
        ]
        + [dma] * 6,
        compiler_params=pltpu.CompilerParams(
            collective_id=0, has_side_effects=True, vmem_limit_bytes=60 * 1024 * 1024
        ),
        name="whole",
    )(design_matrix, targets, linear, diagonal[:, None], lower_code, upper_code)


def solution(mesh):
    in_specs = (
        P("groups", "row"),
        P(("groups", "row"), None),
        P(("groups", "row"), None),
        P(("groups", "row")),
        P(("groups", "row"), None),
        P(("groups", "row"), None),
    )
    out_specs = (P(("groups", "row"), None), P(("groups", "row"), None))
    return jax.shard_map(
        functools.partial(per_device, mesh.shape["row"]),
        mesh=mesh,
        in_specs=in_specs,
        out_specs=out_specs,
        check_vma=False,
    )
```

profile of v0, /device:TPU:0, one launch (start us, length us, event | category | flops | bytes accessed | tf_op | source)
XLA Modules:
  0.0 104.3 jit_solution(10110151814883812473)
XLA Ops:
  0.6 2.7 %copy.8.diag_ref = f32[4096,1]{1,0:T(8,128)} copy(f32[4096,1]{0,1:T(1,128)} %bitcast.1) | data formatting | bytes 32768 | tf_op jit(solution)/shard_map/broadcast_in_dim | solution.py:274
  3.3 96.4 %whole.1 = (f32[4096,128]{1,0:T(8,128)}, f32[4096,128]{1,0:T(8,128)}) custom-call(bf16[512,4096]{1,0:T(8,128)(2,1)} %a_ref.1, f32[32,128]{1,0:T(8,128)} %targets_ref.1, f32[4096,128]{1,0:T(8,128)} %lin_ref.1, f32[4096,1]{1,0:T(8,128)} %copy.8.diag_ref, s32[4096,128]{1,0:T(8,128)} %lo_ref.1, s32[4096,128]{1,0:T(8,128)} %hi_ref.1), custom_call_target="tpu_custom_call" | custom-call | tf_op jit(solution)/shard_map/whole/pallas_call | solution.py:251
  99.8 0.0 copy-start
  99.8 3.2 %copy.11 = f32[4096,128]{1,0:T(8,128)} copy(f32[4096,128]{1,0:T(8,128)} %get-tuple-element.4) | data formatting | bytes 4194304
  103.0 0.0 copy-done
  103.0 1.3 %copy.12 = f32[4096,128]{1,0:T(8,128)} copy(f32[4096,128]{1,0:T(8,128)S(1)} %copy-done) | data formatting | bytes 4194304
Async XLA Ops:
  99.8 3.2 %copy-start = (f32[4096,128]{1,0:T(8,128)S(1)}, f32[4096,128]{1,0:T(8,128)}, u32[]{:S(2)}) copy-start(f32[4096,128]{1,0:T(8,128)} %get-tuple-element.5) | copy-start | bytes 6291460
where the time goes:
time: 105 us; the launch traced here: 104 us
  Pallas kernels  96.4 us (92%)
  local copies, waits for them, and re-layouts  7.2 us (7%)
    pallas_call x1, Pallas kernels, per_device(): pl.pallas_call(functools.partial(whole_kernel, n, min(512, local)), in_sp...  96.4 us
    unnamed x4, local copies, waits for them, and re-layouts  4.52 us
    broadcast_in_dim x1, local copies, waits for them, and re-layouts, per_device(): diagonal[:, None]  2.68 us

commit v1 on v0

v1 whole, which is shorter than its diff:
```python
import functools

import jax
import jax.numpy as jnp
from jax import lax
from jax.experimental import pallas as pl
from jax.experimental.pallas import tpu as pltpu
from jax.sharding import PartitionSpec as P

ITERS = 4
TERM = jnp.bfloat16

rho_plus_lip = 7.0


def solve_small(matrix, rhs):
    count = len(rhs)
    table = [list(line) for line in matrix]
    right = list(rhs)
    for p in range(count):
        for i in range(p + 1, count):
            factor = table[i][p] / table[p][p]
            for j in range(p, count):
                table[i][j] = table[i][j] - factor * table[p][j]
            right[i] = right[i] - factor * right[p]
    result = [None] * count
    for i in reversed(range(count)):
        total = right[i]
        for j in range(i + 1, count):
            total = total - table[i][j] * result[j]
        result[i] = total / table[i][i]
    return result


def mix_weights(gram):
    count = len(gram)
    trace = gram[0][0]
    for i in range(1, count):
        trace = trace + gram[i][i]
    shift = 0.01 * trace / count + 1e-06
    matrix = [[gram[i][j] + (shift if i == j else 0.0) for j in range(count)] for i in range(count)]
    solved = solve_small(matrix, [jnp.ones_like(trace)] * count)
    total = solved[0]
    for i in range(1, count):
        total = total + solved[i]
    return [item / total for item in solved]


def peers_of(n, me):
    if n & (n - 1):
        return [(d, lax.rem(me + d, n), lax.rem(me + n - d, n)) for d in range(n - 1, 0, -1)]
    found = []
    for d in range(n - 1, 0, -1):
        peer = me
        bit = 1
        while bit < n:
            if d & bit:
                peer = peer + bit * (1 - 2 * ((me // bit) % 2))
            bit *= 2
        found.append((d, peer, peer))
    return found


def greet(n, peers):
    barrier = pltpu.get_barrier_semaphore()
    for _, peer, _ in peers:
        pl.semaphore_signal(
            barrier,
            inc=1,
            device_id={"row": peer},
            device_id_type=pl.DeviceIdType.MESH,
        )
    return lambda: pl.semaphore_wait(barrier, n - 1)


def send(src, dst, send_sem, recv_sem, peer):
    copy = pltpu.make_async_remote_copy(
        src_ref=src,
        dst_ref=dst,
        send_sem=send_sem,
        recv_sem=recv_sem,
        device_id={"row": peer},
        device_id_type=pl.DeviceIdType.MESH,
    )
    copy.start()
    return copy


def start_spread(peers, me, mine, whole, send_sem, recv_sem):
    copies = [
        send(mine, whole.at[me], send_sem.at[d], recv_sem.at[d], peer) for d, peer, _ in peers
    ]
    whole[me] = mine[...]
    return copies


def finish(copies):
    for copy in copies:
        copy.wait_recv()
    for copy in copies:
        copy.wait_send()


def chunks(local, size, body):
    def step(i, carry):
        body(pl.ds(pl.multiple_of(i * size, size), size))
        return carry

    lax.fori_loop(0, local // size, step, 0)


def column_sum(x):
    return jnp.sum(x.reshape(-1, 8, x.shape[-1]), axis=0)


def clip(x, lower, upper):
    return jnp.minimum(jnp.maximum(x, lower), upper)


def main_kernel(
    n,
    size,
    a_hbm,
    targets_hbm,
    lin_hbm,
    diag_hbm,
    lo_hbm,
    hi_hbm,
    mapped,
    alpha_ref,
    lower,
    upper,
    a_ref,
    at_ref,
    targets_ref,
    lin_ref,
    diag_ref,
    lo_ref,
    hi_ref,
    step_ref,
    z_ref,
    u_ref,
    changes,
    acc,
    sums,
    terms,
    slots,
    mine,
    misfits,
    part,
    parts,
    grams,
    load_sem,
    send_a,
    recv_a,
    send_b,
    recv_b,
    send_c,
    recv_c,
):
    me = lax.axis_index("row")
    peers = peers_of(n, me)
    local = lin_ref.shape[0]
    k = a_ref.shape[0]

    loads = [
        pltpu.make_async_copy(source, target, load_sem.at[i])
        for i, (source, target) in enumerate(
            [
                (targets_hbm, targets_ref),
                (diag_hbm, diag_ref),
                (a_hbm, a_ref),
                (lo_hbm, lo_ref),
                (hi_hbm, hi_ref),
                (lin_hbm, lin_ref),
            ]
        )
    ]
    for load in loads:
        load.start()
    met = greet(n, peers)
    loads[0].wait()
    mine[...] = (0.0 - targets_ref[...]).astype(jnp.bfloat16)
    met()
    copies = start_spread(peers, me, mine, misfits, send_b, recv_b)

    loads[1].wait()
    lanes = diag_ref.shape[1]
    for i in range(diag_ref.shape[0]):
        line = 1.0 / (rho_plus_lip + diag_ref[i : i + 1, :])
        step_ref[i * lanes : (i + 1) * lanes, :] = jnp.broadcast_to(line, (lanes, lanes)).T
    loads[2].wait()

    def flip(at):
        at_ref[at, :] = a_ref[:, at].T

    chunks(local, size, flip)
    loads[3].wait()
    loads[4].wait()

    def bounds(at):
        lower[at, :] = lo_ref[at, :].astype(jnp.float32) * (1.0 / 64.0)
        upper[at, :] = hi_ref[at, :].astype(jnp.float32) * (1.0 / 64.0)

    chunks(local, size, bounds)
    loads[5].wait()
    acc[...] = jnp.zeros_like(acc)
    sums[...] = jnp.zeros_like(sums)
    finish(copies)

    def gradient_of(at):
        return jnp.dot(
            at_ref[at, :], misfits[...].reshape(k, -1), preferred_element_type=jnp.float32
        )

    def add_product(at, point):
        acc[...] += jnp.dot(
            a_ref[:, at], point.astype(jnp.bfloat16), preferred_element_type=jnp.float32
        )

    def start(at):
        moved = 0.0 - step_ref[at, :] * (gradient_of(at) + lin_ref[at, :])
        boxed = clip(moved, lower[at, :], upper[at, :])
        scaled = moved - boxed
        mapped[0, 0, at, :] = boxed
        mapped[0, 1, at, :] = scaled
        sums[ITERS] += column_sum(boxed * boxed + scaled * scaled)
        add_product(at, boxed - scaled)

    chunks(local, size, start)

    for iteration in range(1, ITERS):
        count = iteration + 1
        last = iteration == ITERS - 1
        terms[...] = acc[...].reshape(terms.shape).astype(terms.dtype)
        copies = [
            send(terms.at[peer], slots.at[d - 1], send_a.at[d], recv_a.at[d], peer)
            for d, peer, _ in peers
        ]
        total = terms[me].astype(jnp.float32) - targets_ref[...]
        for copy, (d, _, _) in reversed(list(zip(copies, peers))):
            copy.wait_recv()
            total = total + slots[d - 1].astype(jnp.float32)
        mine[...] = total.astype(jnp.bfloat16)
        spread = start_spread(peers, me, mine, misfits, send_b, recv_b)
        for copy in copies:
            copy.wait_send()
        finish(spread)

        def advance(at):
            if iteration == 1:
                z, u = mapped[0, 0, at, :], mapped[0, 1, at, :]
            else:
                z, u = z_ref[at, :], u_ref[at, :]
            moved = step_ref[at, :] * (
                rho_plus_lip * (z - u) - lin_ref[at, :] - gradient_of(at)
            )
            raw = moved + u
            boxed = clip(raw, lower[at, :], upper[at, :])
            scaled = raw - boxed
            mapped[iteration, 0, at, :] = boxed
            mapped[iteration, 1, at, :] = scaled
            cz, cu = boxed - z, scaled - u
            if not last:
                changes[iteration - 1, 0, at, :] = cz
                changes[iteration - 1, 1, at, :] = cu
            sums[0] += column_sum(cz * mapped[0, 0, at, :] + cu * mapped[0, 1, at, :])
            for i in range(1, iteration):
                sums[i] += column_sum(
                    cz * changes[i - 1, 0, at, :] + cu * changes[i - 1, 1, at, :]
                )
            sums[iteration] += column_sum(cz * cz + cu * cu)

        chunks(local, size, advance)

        kept = list(range(count)) + ([ITERS] if iteration == 1 else [])
        for i in kept:
            row = i if i < ITERS else ITERS - 1
            part[row : row + 1, :] = jnp.sum(sums[i], axis=0, keepdims=True)
        spread = start_spread(peers, me, part, parts, send_c, recv_c)
        sums[...] = jnp.zeros_like(sums)
        acc[...] = jnp.zeros_like(acc)
        finish(spread)
        whole = parts[0]
        for i in range(1, n):
            whole = whole + parts[i]
        grams[iteration - 1] = whole

        gram = [[None] * count for _ in range(count)]
        gram[0][0] = grams[0, ITERS - 1 : ITERS, :]
        for i in range(1, count):
            for j in range(i + 1):
                gram[i][j] = gram[j][i] = grams[i - 1, j : j + 1, :]
        for i, row in enumerate(mix_weights(gram)):
            alpha_ref[i : i + 1, :] = row

        if last:
            break

        def mix(at):
            z = alpha_ref[0:1, :] * mapped[0, 0, at, :]
            u = alpha_ref[0:1, :] * mapped[0, 1, at, :]
            for i in range(1, count):
                z = z + alpha_ref[i : i + 1, :] * mapped[i, 0, at, :]
                u = u + alpha_ref[i : i + 1, :] * mapped[i, 1, at, :]
            z = clip(z, lower[at, :], upper[at, :])
            z_ref[at, :] = z
            u_ref[at, :] = u
            add_product(at, z - u)

        chunks(local, size, mix)


def mix_kernel(size, mapped, alpha_ref, lower, upper, z_hbm, u_hbm, z_ref, u_ref, sem):
    local = lower.shape[0]
    steps = local // size
    copies = []
    for step in range(steps):
        at = pl.ds(step * size, size)
        z = alpha_ref[0:1, :] * mapped[0, 0, at, :]
        u = alpha_ref[0:1, :] * mapped[0, 1, at, :]
        for i in range(1, ITERS):
            z = z + alpha_ref[i : i + 1, :] * mapped[i, 0, at, :]
            u = u + alpha_ref[i : i + 1, :] * mapped[i, 1, at, :]
        z_ref[at, :] = clip(z, lower[at, :], upper[at, :])
        u_ref[at, :] = u
        for j, (src, dst) in enumerate([(z_ref, z_hbm), (u_ref, u_hbm)]):
            copy = pltpu.make_async_copy(src.at[at, :], dst.at[at, :], sem.at[j, step])
            copy.start()
            copies.append(copy)
    for copy in copies:
        copy.wait()


def per_device(n, design_matrix, targets, linear, diagonal, lower_code, upper_code):
    k = design_matrix.shape[0]
    local, s = linear.shape
    kr = k // n
    size = min(512, local)
    big = (local, s)
    lines = diagonal.reshape(local // s, s)
    vmem = pl.BlockSpec(memory_space=pltpu.VMEM)
    hbm = pl.BlockSpec(memory_space=pl.ANY)
    dma = pltpu.SemaphoreType.DMA((n,))
    mapped, alpha, lower, upper = pl.pallas_call(
        functools.partial(main_kernel, n, size),
        in_specs=[hbm] * 6,
        out_specs=[vmem] * 4,
        out_shape=[
            pltpu.VMEM((ITERS, 2, local, s), jnp.float32),
            pltpu.VMEM((8, s), jnp.float32),
            pltpu.VMEM(big, jnp.float32),
            pltpu.VMEM(big, jnp.float32),
        ],
        scratch_shapes=[
            pltpu.VMEM((k, local), jnp.bfloat16),
            pltpu.VMEM((local, k), jnp.bfloat16),
            pltpu.VMEM((kr, s), jnp.float32),
            pltpu.VMEM(big, jnp.float32),
            pltpu.VMEM((local // s, s), jnp.float32),
            pltpu.VMEM(big, jnp.int32),
            pltpu.VMEM(big, jnp.int32),
            pltpu.VMEM(big, jnp.float32),
            pltpu.VMEM(big, jnp.float32),
            pltpu.VMEM(big, jnp.float32),
            pltpu.VMEM((ITERS - 2, 2, local, s), jnp.float32),
            pltpu.VMEM((k, s), jnp.float32),
            pltpu.VMEM((ITERS + 1, 8, s), jnp.float32),
            pltpu.VMEM((n, kr, s), TERM),
            pltpu.VMEM((n - 1, kr, s), TERM),
            pltpu.VMEM((kr, s), jnp.bfloat16),
            pltpu.VMEM((n, kr, s), jnp.bfloat16),
            pltpu.VMEM((ITERS, s), jnp.float32),
            pltpu.VMEM((n, ITERS, s), jnp.float32),
            pltpu.VMEM((ITERS - 1, ITERS, s), jnp.float32),
            pltpu.SemaphoreType.DMA((6,)),
        ]
        + [dma] * 6,
        compiler_params=pltpu.CompilerParams(
            collective_id=0, has_side_effects=True, vmem_limit_bytes=36 * 1024 * 1024
        ),
        name="main",
    )(design_matrix, targets, linear, lines, lower_code, upper_code)
    return pl.pallas_call(
        functools.partial(mix_kernel, size),
        in_specs=[vmem] * 4,
        out_specs=[hbm] * 2,
        out_shape=[jax.ShapeDtypeStruct(big, jnp.float32)] * 2,
        scratch_shapes=[
            pltpu.VMEM(big, jnp.float32),
            pltpu.VMEM(big, jnp.float32),
            pltpu.SemaphoreType.DMA((2, local // size)),
        ],
        compiler_params=pltpu.CompilerParams(vmem_limit_bytes=8 * 1024 * 1024),
        name="last_mix",
    )(mapped, alpha, lower, upper)


def solution(mesh):
    in_specs = (
        P("groups", "row"),
        P(("groups", "row"), None),
        P(("groups", "row"), None),
        P(("groups", "row")),
        P(("groups", "row"), None),
        P(("groups", "row"), None),
    )
    out_specs = (P(("groups", "row"), None), P(("groups", "row"), None))
    return jax.shard_map(
        functools.partial(per_device, mesh.shape["row"]),
        mesh=mesh,
        in_specs=in_specs,
        out_specs=out_specs,
        check_vma=False,
    )
```

time: 105 us -> 77.4 us (0.74)
  Pallas kernels: 96.4 us -> 76.5 us
  local copies, waits for them, and re-layouts: 7.2 us -> 0 us
    pallas_call x1 -> x2, Pallas kernels: 96.4 us -> 76.5 us  [the longest x1 74.3 us: per_device(): pl.pallas_call(functools.partial(main_kernel, n, size), in_specs=[hbm] *...]
    unnamed x4 -> x0, local copies, waits for them, and re-layouts: 4.52 us -> none
    broadcast_in_dim x1 -> x0, local copies, waits for them, and re-layouts: 2.68 us -> none  [per_device(): diagonal[:, None]]
where the time goes in v1:
time: 77.4 us; the launch traced here: 77.2 us
  Pallas kernels  76.5 us (99%)
    pallas_call x1, Pallas kernels, per_device(): pl.pallas_call(functools.partial(main_kernel, n, size), in_specs=[hbm] *...  74.3 us
    pallas_call x1, Pallas kernels, per_device(): pl.pallas_call(functools.partial(mix_kernel, size), in_specs=[vmem] * 4,...  2.24 us

profile of v1, /device:TPU:0, one launch (start us, length us, event | category | flops | bytes accessed | tf_op | source)
XLA Modules:
  0.0 77.2 jit_solution(16669340462801060518)
XLA Ops:
  0.6 74.3 %main.1 = (f32[4,2,4096,128]{3,2,1,0:T(8,128)S(1)}, f32[8,128]{1,0:T(8,128)S(1)}, f32[4096,128]{1,0:T(8,128)S(1)}, f32[4096,128]{1,0:T(8,128)S(1)}) custom-call(bf16[512,4096]{1,0:T(8,128)(2,1)} %a_hbm.1, f32[32,128]{1,0:T(8,128)} %targets_hbm.1, f32[4096,128]{1,0:T(8,128)} %lin_hbm.1, f32[32,128]{1,0:T(8,128)} %bitcast.1, s32[4096,128]{1,0:T(8,128)} %lo_hbm.1, ...), custom_call_target="tpu_custom_call" | custom-call | tf_op jit(solution)/shard_map/main/pallas_call | solution.py:345
  74.9 2.2 %last_mix.1 = (f32[4096,128]{1,0:T(8,128)}, f32[4096,128]{1,0:T(8,128)}) custom-call(f32[4,2,4096,128]{3,2,1,0:T(8,128)S(1)} %get-tuple-element.6.mapped, f32[8,128]{1,0:T(8,128)S(1)} %get-tuple-element.7.alpha_ref, f32[4096,128]{1,0:T(8,128)S(1)} %get-tuple-element.8.lower, f32[4096,128]{1,0:T(8,128)S(1)} %get-tuple-element.9.upper), custom_call_target="tpu_custom_call" | custom-call | tf_op jit(solution)/shard_map/last_mix/pallas_call | solution.py:384

commit v2 on v1

--- a/solution.py
+++ b/solution.py
@@ -17,10 +17,12 @@
     count = len(rhs)
     table = [list(line) for line in matrix]
     right = list(rhs)
+    inverse = []
     for p in range(count):
+        inverse.append(1.0 / table[p][p])
         for i in range(p + 1, count):
-            factor = table[i][p] / table[p][p]
-            for j in range(p, count):
+            factor = table[i][p] * inverse[p]
+            for j in range(p + 1, count):
                 table[i][j] = table[i][j] - factor * table[p][j]
             right[i] = right[i] - factor * right[p]
     result = [None] * count
@@ -28,7 +30,7 @@
         total = right[i]
         for j in range(i + 1, count):
             total = total - table[i][j] * result[j]
-        result[i] = total / table[i][i]
+        result[i] = total * inverse[i]
     return result
 
 
@@ -43,12 +45,11 @@
     total = solved[0]
     for i in range(1, count):
         total = total + solved[i]
-    return [item / total for item in solved]
+    scale = 1.0 / total
+    return [item * scale for item in solved]
 
 
 def peers_of(n, me):
-    if n & (n - 1):
-        return [(d, lax.rem(me + d, n), lax.rem(me + n - d, n)) for d in range(n - 1, 0, -1)]
     found = []
     for d in range(n - 1, 0, -1):
         peer = me
@@ -57,13 +58,13 @@
             if d & bit:
                 peer = peer + bit * (1 - 2 * ((me // bit) % 2))
             bit *= 2
-        found.append((d, peer, peer))
+        found.append((d, peer))
     return found
 
 
 def greet(n, peers):
     barrier = pltpu.get_barrier_semaphore()
-    for _, peer, _ in peers:
+    for _, peer in peers:
         pl.semaphore_signal(
             barrier,
             inc=1,
@@ -88,7 +89,7 @@
 
 def start_spread(peers, me, mine, whole, send_sem, recv_sem):
     copies = [
-        send(mine, whole.at[me], send_sem.at[d], recv_sem.at[d], peer) for d, peer, _ in peers
+        send(mine, whole.at[me], send_sem.at[d], recv_sem.at[d], peer) for d, peer in peers
     ]
     whole[me] = mine[...]
     return copies
@@ -135,6 +136,7 @@
     targets_ref,
     lin_ref,
     diag_ref,
+    base_ref,
     lo_ref,
     hi_ref,
     step_ref,
@@ -145,6 +147,8 @@
     sums,
     terms,
     slots,
+    sent,
+    running,
     mine,
     misfits,
     part,
@@ -206,56 +210,96 @@
     loads[5].wait()
     acc[...] = jnp.zeros_like(acc)
     sums[...] = jnp.zeros_like(sums)
-    finish(copies)
-
-    def gradient_of(at):
+    half = me // (n // 2)
+
+    def gradient_of(at, which):
+        rows = pl.ds(pl.multiple_of(which * (n // 2), n // 2), n // 2)
+        columns = pl.ds(pl.multiple_of(which * (k // 2), k // 2), k // 2)
         return jnp.dot(
-            at_ref[at, :], misfits[...].reshape(k, -1), preferred_element_type=jnp.float32
+            at_ref[at, columns],
+            misfits[rows].reshape(k // 2, -1),
+            preferred_element_type=jnp.float32,
         )
 
     def add_product(at, point):
         acc[...] += jnp.dot(
-            a_ref[:, at], point.astype(jnp.bfloat16), preferred_element_type=jnp.float32
+            point.astype(jnp.bfloat16).T, at_ref[at, :], preferred_element_type=jnp.float32
         )
 
+    def near(at):
+        base_ref[at, :] -= step_ref[at, :] * gradient_of(at, half)
+
+    def gather_near(copies):
+        for copy, (d, _) in zip(copies, peers):
+            if d < n // 2:
+                copy.wait_recv()
+        chunks(local, size, near)
+        for copy, (d, _) in zip(copies, peers):
+            if d >= n // 2:
+                copy.wait_recv()
+
+    def raw_of(at):
+        return base_ref[at, :] - step_ref[at, :] * gradient_of(at, 1 - half)
+
+    def base(at):
+        base_ref[at, :] = 0.0 - step_ref[at, :] * lin_ref[at, :]
+
+    chunks(local, size, base)
+    gather_near(copies)
+
     def start(at):
-        moved = 0.0 - step_ref[at, :] * (gradient_of(at) + lin_ref[at, :])
-        boxed = clip(moved, lower[at, :], upper[at, :])
-        scaled = moved - boxed
+        raw = raw_of(at)
+        boxed = clip(raw, lower[at, :], upper[at, :])
+        scaled = raw - boxed
         mapped[0, 0, at, :] = boxed
         mapped[0, 1, at, :] = scaled
         sums[ITERS] += column_sum(boxed * boxed + scaled * scaled)
         add_product(at, boxed - scaled)
 
     chunks(local, size, start)
+    for copy in copies:
+        copy.wait_send()
 
     for iteration in range(1, ITERS):
         count = iteration + 1
         last = iteration == ITERS - 1
-        terms[...] = acc[...].reshape(terms.shape).astype(terms.dtype)
+        rounded = acc[...].astype(terms.dtype)
+        terms[...] = rounded.T.reshape(terms.shape)
         copies = [
             send(terms.at[peer], slots.at[d - 1], send_a.at[d], recv_a.at[d], peer)
-            for d, peer, _ in peers
+            for d, peer in peers
         ]
-        total = terms[me].astype(jnp.float32) - targets_ref[...]
-        for copy, (d, _, _) in reversed(list(zip(copies, peers))):
+        if iteration == 1:
+            sent[...] = rounded.astype(jnp.float32)
+            total = terms[me].astype(jnp.float32) - targets_ref[...]
+        else:
+            sent[...] += rounded.astype(jnp.float32)
+            total = terms[me].astype(jnp.float32) + running[...]
+        acc[...] = 0.0 - sent[...]
+
+        def state(at):
+            if iteration == 1:
+                return mapped[0, 0, at, :], mapped[0, 1, at, :]
+            return z_ref[at, :], u_ref[at, :]
+
+        def base(at):
+            z, u = state(at)
+            base_ref[at, :] = step_ref[at, :] * (rho_plus_lip * (z - u) - lin_ref[at, :]) + u
+
+        chunks(local, size, base)
+        for copy, (d, _) in reversed(list(zip(copies, peers))):
             copy.wait_recv()
             total = total + slots[d - 1].astype(jnp.float32)
+        running[...] = total
         mine[...] = total.astype(jnp.bfloat16)
         spread = start_spread(peers, me, mine, misfits, send_b, recv_b)
         for copy in copies:
             copy.wait_send()
-        finish(spread)
+        gather_near(spread)
 
         def advance(at):
-            if iteration == 1:
-                z, u = mapped[0, 0, at, :], mapped[0, 1, at, :]
-            else:
-                z, u = z_ref[at, :], u_ref[at, :]
-            moved = step_ref[at, :] * (
-                rho_plus_lip * (z - u) - lin_ref[at, :] - gradient_of(at)
-            )
-            raw = moved + u
+            z, u = state(at)
+            raw = raw_of(at)
             boxed = clip(raw, lower[at, :], upper[at, :])
             scaled = raw - boxed
             mapped[iteration, 0, at, :] = boxed
@@ -272,6 +316,8 @@
             sums[iteration] += column_sum(cz * cz + cu * cu)
 
         chunks(local, size, advance)
+        for copy in spread:
+            copy.wait_send()
 
         kept = list(range(count)) + ([ITERS] if iteration == 1 else [])
         for i in kept:
@@ -279,7 +325,6 @@
             part[row : row + 1, :] = jnp.sum(sums[i], axis=0, keepdims=True)
         spread = start_spread(peers, me, part, parts, send_c, recv_c)
         sums[...] = jnp.zeros_like(sums)
-        acc[...] = jnp.zeros_like(acc)
         finish(spread)
         whole = parts[0]
         for i in range(1, n):
@@ -336,7 +381,7 @@
     k = design_matrix.shape[0]
     local, s = linear.shape
     kr = k // n
-    size = min(512, local)
+    size = min(2048, local)
     big = (local, s)
     lines = diagonal.reshape(local // s, s)
     vmem = pl.BlockSpec(memory_space=pltpu.VMEM)
@@ -358,16 +403,19 @@
             pltpu.VMEM((kr, s), jnp.float32),
             pltpu.VMEM(big, jnp.float32),
             pltpu.VMEM((local // s, s), jnp.float32),
+            pltpu.VMEM(big, jnp.float32),
             pltpu.VMEM(big, jnp.int32),
             pltpu.VMEM(big, jnp.int32),
             pltpu.VMEM(big, jnp.float32),
             pltpu.VMEM(big, jnp.float32),
             pltpu.VMEM(big, jnp.float32),
             pltpu.VMEM((ITERS - 2, 2, local, s), jnp.float32),
-            pltpu.VMEM((k, s), jnp.float32),
+            pltpu.VMEM((s, k), jnp.float32),
             pltpu.VMEM((ITERS + 1, 8, s), jnp.float32),
             pltpu.VMEM((n, kr, s), TERM),
             pltpu.VMEM((n - 1, kr, s), TERM),
+            pltpu.VMEM((s, k), jnp.float32),
+            pltpu.VMEM((kr, s), jnp.float32),
             pltpu.VMEM((kr, s), jnp.bfloat16),
             pltpu.VMEM((n, kr, s), jnp.bfloat16),
             pltpu.VMEM((ITERS, s), jnp.float32),
@@ -377,7 +425,7 @@
         ]
         + [dma] * 6,
         compiler_params=pltpu.CompilerParams(
-            collective_id=0, has_side_effects=True, vmem_limit_bytes=36 * 1024 * 1024
+            collective_id=0, has_side_effects=True, vmem_limit_bytes=38 * 1024 * 1024
         ),
         name="main",
     )(design_matrix, targets, linear, lines, lower_code, upper_code)

time: 77.4 us -> 68.8 us (0.89)
  Pallas kernels: 76.5 us -> 68 us
    pallas_call x1, Pallas kernels: 74.3 us -> 65.6 us  [per_device(): pl.pallas_call(functools.partial(main_kernel, n, size), in_specs=[hbm] *...]
where the time goes in v2:
time: 68.8 us; the launch traced here: 68.6 us
  Pallas kernels  68 us (99%)
    pallas_call x1, Pallas kernels, per_device(): pl.pallas_call(functools.partial(main_kernel, n, size), in_specs=[hbm] *...  65.6 us
    pallas_call x1, Pallas kernels, per_device(): pl.pallas_call(functools.partial(mix_kernel, size), in_specs=[vmem] * 4,...  2.41 us

profile of v2, /device:TPU:0, one launch (start us, length us, event | category | flops | bytes accessed | tf_op | source)
XLA Modules:
  0.0 68.6 jit_solution(18005917895185322443)
XLA Ops:
  0.6 65.6 %main.1 = (f32[4,2,4096,128]{3,2,1,0:T(8,128)S(1)}, f32[8,128]{1,0:T(8,128)S(1)}, f32[4096,128]{1,0:T(8,128)S(1)}, f32[4096,128]{1,0:T(8,128)S(1)}) custom-call(bf16[512,4096]{1,0:T(8,128)(2,1)} %a_hbm.1, f32[32,128]{1,0:T(8,128)} %targets_hbm.1, f32[4096,128]{1,0:T(8,128)} %lin_hbm.1, f32[32,128]{1,0:T(8,128)} %bitcast.1, s32[4096,128]{1,0:T(8,128)} %lo_hbm.1, ...), custom_call_target="tpu_custom_call" | custom-call | tf_op jit(solution)/shard_map/main/pallas_call | solution.py:390
  66.2 2.4 %last_mix.1 = (f32[4096,128]{1,0:T(8,128)}, f32[4096,128]{1,0:T(8,128)}) custom-call(f32[4,2,4096,128]{3,2,1,0:T(8,128)S(1)} %get-tuple-element.6.mapped, f32[8,128]{1,0:T(8,128)S(1)} %get-tuple-element.7.alpha_ref, f32[4096,128]{1,0:T(8,128)S(1)} %get-tuple-element.8.lower, f32[4096,128]{1,0:T(8,128)S(1)} %get-tuple-element.9.upper), custom_call_target="tpu_custom_call" | custom-call | tf_op jit(solution)/shard_map/last_mix/pallas_call | solution.py:432

commit v3 on v2

--- a/solution.py
+++ b/solution.py
@@ -108,6 +108,11 @@
         return carry
 
     lax.fori_loop(0, local // size, step, 0)
+
+
+def pieces(local, size, body):
+    for i in range(local // size):
+        body(pl.ds(i * size, size))
 
 
 def column_sum(x):
@@ -148,6 +153,8 @@
     terms,
     slots,
     sent,
+    rounded,
+    flat,
     running,
     mine,
     misfits,
@@ -221,10 +228,35 @@
             preferred_element_type=jnp.float32,
         )
 
+    def columns_of(which):
+        return pl.ds(pl.multiple_of(which * (k // 2), k // 2), k // 2)
+
     def add_product(at, point):
-        acc[...] += jnp.dot(
-            point.astype(jnp.bfloat16).T, at_ref[at, :], preferred_element_type=jnp.float32
+        turned = point.astype(jnp.bfloat16).T
+        flat[:, at] = turned
+        columns = columns_of(1 - half)
+        acc[:, columns] += jnp.dot(
+            turned, at_ref[at, columns], preferred_element_type=jnp.float32
         )
+
+    def send_terms(which, chosen):
+        columns = columns_of(which)
+        value = acc[:, columns].astype(terms.dtype)
+        rounded[:, columns] = value
+        rows = pl.ds(pl.multiple_of(which * (n // 2), n // 2), n // 2)
+        terms[rows] = value.T.reshape((n // 2,) + terms.shape[1:])
+        return [
+            send(terms.at[peer], slots.at[d - 1], send_a.at[d], recv_a.at[d], peer)
+            for d, peer in chosen
+        ]
+
+    def start_sum():
+        copies = send_terms(1 - half, [peer for peer in peers if peer[0] >= n // 2])
+        columns = columns_of(half)
+        acc[:, columns] += jnp.dot(
+            flat[...], at_ref[:, columns], preferred_element_type=jnp.float32
+        )
+        return copies + send_terms(half, [peer for peer in peers if peer[0] < n // 2])
 
     def near(at):
         base_ref[at, :] -= step_ref[at, :] * gradient_of(at, half)
@@ -263,17 +295,12 @@
     for iteration in range(1, ITERS):
         count = iteration + 1
         last = iteration == ITERS - 1
-        rounded = acc[...].astype(terms.dtype)
-        terms[...] = rounded.T.reshape(terms.shape)
-        copies = [
-            send(terms.at[peer], slots.at[d - 1], send_a.at[d], recv_a.at[d], peer)
-            for d, peer in peers
-        ]
+        copies = start_sum()
         if iteration == 1:
-            sent[...] = rounded.astype(jnp.float32)
+            sent[...] = rounded[...].astype(jnp.float32)
             total = terms[me].astype(jnp.float32) - targets_ref[...]
         else:
-            sent[...] += rounded.astype(jnp.float32)
+            sent[...] += rounded[...].astype(jnp.float32)
             total = terms[me].astype(jnp.float32) + running[...]
         acc[...] = 0.0 - sent[...]
 
@@ -305,9 +332,6 @@
             mapped[iteration, 0, at, :] = boxed
             mapped[iteration, 1, at, :] = scaled
             cz, cu = boxed - z, scaled - u
-            if not last:
-                changes[iteration - 1, 0, at, :] = cz
-                changes[iteration - 1, 1, at, :] = cu
             sums[0] += column_sum(cz * mapped[0, 0, at, :] + cu * mapped[0, 1, at, :])
             for i in range(1, iteration):
                 sums[i] += column_sum(
@@ -315,7 +339,7 @@
                 )
             sums[iteration] += column_sum(cz * cz + cu * cu)
 
-        chunks(local, size, advance)
+        pieces(local, min(512, local), advance)
         for copy in spread:
             copy.wait_send()
 
@@ -325,6 +349,13 @@
             part[row : row + 1, :] = jnp.sum(sums[i], axis=0, keepdims=True)
         spread = start_spread(peers, me, part, parts, send_c, recv_c)
         sums[...] = jnp.zeros_like(sums)
+
+        def keep(at):
+            for j, before in enumerate(state(at)):
+                changes[iteration - 1, j, at, :] = mapped[iteration, j, at, :] - before
+
+        if not last:
+            chunks(local, size, keep)
         finish(spread)
         whole = parts[0]
         for i in range(1, n):
@@ -353,7 +384,7 @@
             u_ref[at, :] = u
             add_product(at, z - u)
 
-        chunks(local, size, mix)
+        pieces(local, min(512, local), mix)
 
 
 def mix_kernel(size, mapped, alpha_ref, lower, upper, z_hbm, u_hbm, z_ref, u_ref, sem):
@@ -415,6 +446,8 @@
             pltpu.VMEM((n, kr, s), TERM),
             pltpu.VMEM((n - 1, kr, s), TERM),
             pltpu.VMEM((s, k), jnp.float32),
+            pltpu.VMEM((s, k), TERM),
+            pltpu.VMEM((s, local), jnp.bfloat16),
             pltpu.VMEM((kr, s), jnp.float32),
             pltpu.VMEM((kr, s), jnp.bfloat16),
             pltpu.VMEM((n, kr, s), jnp.bfloat16),
@@ -425,19 +458,19 @@
         ]
         + [dma] * 6,
         compiler_params=pltpu.CompilerParams(
-            collective_id=0, has_side_effects=True, vmem_limit_bytes=38 * 1024 * 1024
+            collective_id=0, has_side_effects=True, vmem_limit_bytes=40 * 1024 * 1024
         ),
         name="main",
     )(design_matrix, targets, linear, lines, lower_code, upper_code)
     return pl.pallas_call(
-        functools.partial(mix_kernel, size),
+        functools.partial(mix_kernel, min(512, local)),
         in_specs=[vmem] * 4,
         out_specs=[hbm] * 2,
         out_shape=[jax.ShapeDtypeStruct(big, jnp.float32)] * 2,
         scratch_shapes=[
             pltpu.VMEM(big, jnp.float32),
             pltpu.VMEM(big, jnp.float32),
-            pltpu.SemaphoreType.DMA((2, local // size)),
+            pltpu.SemaphoreType.DMA((2, local // min(512, local))),
         ],
         compiler_params=pltpu.CompilerParams(vmem_limit_bytes=8 * 1024 * 1024),
         name="last_mix",

time: 68.8 us -> 66.8 us (0.971)
  Pallas kernels: 68 us -> 65.8 us
    pallas_call x1, Pallas kernels: 65.6 us -> 63.5 us  [per_device(): pl.pallas_call(functools.partial(main_kernel, n, size), in_specs=[hbm] *...]
where the time goes in v3:
time: 66.8 us; the launch traced here: 66.6 us
  Pallas kernels  65.8 us (99%)
  between operations  0.8 us (1%)
    pallas_call x1, Pallas kernels, per_device(): pl.pallas_call(functools.partial(main_kernel, n, size), in_specs=[hbm] *...  63.5 us
    pallas_call x1, Pallas kernels, per_device(): pl.pallas_call(functools.partial(mix_kernel, min(512, local)), in_specs=[...  2.24 us

profile of v3, /device:TPU:0, one launch (start us, length us, event | category | flops | bytes accessed | tf_op | source)
XLA Modules:
  0.0 66.6 jit_solution(12957129508129015439)
XLA Ops:
  0.6 63.5 %main.1 = (f32[4,2,4096,128]{3,2,1,0:T(8,128)S(1)}, f32[8,128]{1,0:T(8,128)S(1)}, f32[4096,128]{1,0:T(8,128)S(1)}, f32[4096,128]{1,0:T(8,128)S(1)}) custom-call(bf16[512,4096]{1,0:T(8,128)(2,1)} %a_hbm.1, f32[32,128]{1,0:T(8,128)} %targets_hbm.1, f32[4096,128]{1,0:T(8,128)} %lin_hbm.1, f32[32,128]{1,0:T(8,128)} %bitcast.1, s32[4096,128]{1,0:T(8,128)} %lo_hbm.1, ...), custom_call_target="tpu_custom_call" | custom-call | tf_op jit(solution)/shard_map/main/pallas_call | solution.py:421
  64.2 2.2 %last_mix.1 = (f32[4096,128]{1,0:T(8,128)}, f32[4096,128]{1,0:T(8,128)}) custom-call(f32[4,2,4096,128]{3,2,1,0:T(8,128)S(1)} %get-tuple-element.6.mapped, f32[8,128]{1,0:T(8,128)S(1)} %get-tuple-element.7.alpha_ref, f32[4096,128]{1,0:T(8,128)S(1)} %get-tuple-element.8.lower, f32[4096,128]{1,0:T(8,128)S(1)} %get-tuple-element.9.upper), custom_call_target="tpu_custom_call" | custom-call | tf_op jit(solution)/shard_map/last_mix/pallas_call | solution.py:465

commit v4 on v3

--- a/solution.py
+++ b/solution.py
@@ -93,13 +93,6 @@
     ]
     whole[me] = mine[...]
     return copies
-
-
-def finish(copies):
-    for copy in copies:
-        copy.wait_recv()
-    for copy in copies:
-        copy.wait_send()
 
 
 def chunks(local, size, body):
@@ -288,14 +281,15 @@
         sums[ITERS] += column_sum(boxed * boxed + scaled * scaled)
         add_product(at, boxed - scaled)
 
-    chunks(local, size, start)
-    for copy in copies:
-        copy.wait_send()
+    pieces(local, min(1024, local), start)
+    spread = copies
 
     for iteration in range(1, ITERS):
         count = iteration + 1
         last = iteration == ITERS - 1
         copies = start_sum()
+        for copy in spread if iteration == 1 else held:
+            copy.wait_send()
         if iteration == 1:
             sent[...] = rounded[...].astype(jnp.float32)
             total = terms[me].astype(jnp.float32) - targets_ref[...]
@@ -340,14 +334,15 @@
             sums[iteration] += column_sum(cz * cz + cu * cu)
 
         pieces(local, min(512, local), advance)
-        for copy in spread:
-            copy.wait_send()
+        gathered = spread
 
         kept = list(range(count)) + ([ITERS] if iteration == 1 else [])
         for i in kept:
             row = i if i < ITERS else ITERS - 1
             part[row : row + 1, :] = jnp.sum(sums[i], axis=0, keepdims=True)
         spread = start_spread(peers, me, part, parts, send_c, recv_c)
+        for copy in gathered:
+            copy.wait_send()
         sums[...] = jnp.zeros_like(sums)
 
         def keep(at):
@@ -356,7 +351,8 @@
 
         if not last:
             chunks(local, size, keep)
-        finish(spread)
+        for copy in reversed(spread):
+            copy.wait_recv()
         whole = parts[0]
         for i in range(1, n):
             whole = whole + parts[i]
@@ -371,6 +367,8 @@
             alpha_ref[i : i + 1, :] = row
 
         if last:
+            for copy in spread:
+                copy.wait_send()
             break
 
         def mix(at):
@@ -385,6 +383,7 @@
             add_product(at, z - u)
 
         pieces(local, min(512, local), mix)
+        held = spread
 
 
 def mix_kernel(size, mapped, alpha_ref, lower, upper, z_hbm, u_hbm, z_ref, u_ref, sem):

time: 66.8 us -> 66.4 us (level)
  no operation moved by 1% of the time
where the time goes in v4:
time: 66.4 us; the launch traced here: 66.1 us
  Pallas kernels  65.3 us (98%)
  between operations  0.8 us (1%)
    pallas_call x1, Pallas kernels, per_device(): pl.pallas_call(functools.partial(main_kernel, n, size), in_specs=[hbm] *...  63.1 us
    pallas_call x1, Pallas kernels, per_device(): pl.pallas_call(functools.partial(mix_kernel, min(512, local)), in_specs=[...  2.24 us

profile of v4, /device:TPU:0, one launch (start us, length us, event | category | flops | bytes accessed | tf_op | source)
XLA Modules:
  0.0 66.1 jit_solution(2078836019919963586)
XLA Ops:
  0.6 63.1 %main.1 = (f32[4,2,4096,128]{3,2,1,0:T(8,128)S(1)}, f32[8,128]{1,0:T(8,128)S(1)}, f32[4096,128]{1,0:T(8,128)S(1)}, f32[4096,128]{1,0:T(8,128)S(1)}) custom-call(bf16[512,4096]{1,0:T(8,128)(2,1)} %a_hbm.1, f32[32,128]{1,0:T(8,128)} %targets_hbm.1, f32[4096,128]{1,0:T(8,128)} %lin_hbm.1, f32[32,128]{1,0:T(8,128)} %bitcast.1, s32[4096,128]{1,0:T(8,128)} %lo_hbm.1, ...), custom_call_target="tpu_custom_call" | custom-call | tf_op jit(solution)/shard_map/main/pallas_call | solution.py:420
  63.7 2.2 %last_mix.1 = (f32[4096,128]{1,0:T(8,128)}, f32[4096,128]{1,0:T(8,128)}) custom-call(f32[4,2,4096,128]{3,2,1,0:T(8,128)S(1)} %get-tuple-element.6.mapped, f32[8,128]{1,0:T(8,128)S(1)} %get-tuple-element.7.alpha_ref, f32[4096,128]{1,0:T(8,128)S(1)} %get-tuple-element.8.lower, f32[4096,128]{1,0:T(8,128)S(1)} %get-tuple-element.9.upper), custom_call_target="tpu_custom_call" | custom-call | tf_op jit(solution)/shard_map/last_mix/pallas_call | solution.py:464

commit v5 on v4

--- a/solution.py
+++ b/solution.py
@@ -135,6 +135,8 @@
     lin_ref,
     diag_ref,
     base_ref,
+    low_ref,
+    high_ref,
     lo_ref,
     hi_ref,
     step_ref,
@@ -305,7 +307,10 @@
 
         def base(at):
             z, u = state(at)
-            base_ref[at, :] = step_ref[at, :] * (rho_plus_lip * (z - u) - lin_ref[at, :]) + u
+            step = step_ref[at, :]
+            base_ref[at, :] = step * (rho_plus_lip * (z - u) - lin_ref[at, :]) + (u - z)
+            low_ref[at, :] = lower[at, :] - z
+            high_ref[at, :] = upper[at, :] - z
 
         chunks(local, size, base)
         for copy, (d, _) in reversed(list(zip(copies, peers))):
@@ -319,13 +324,15 @@
         gather_near(spread)
 
         def advance(at):
-            z, u = state(at)
-            raw = raw_of(at)
-            boxed = clip(raw, lower[at, :], upper[at, :])
-            scaled = raw - boxed
-            mapped[iteration, 0, at, :] = boxed
-            mapped[iteration, 1, at, :] = scaled
-            cz, cu = boxed - z, scaled - u
+            shifted = raw_of(at)
+            cz = clip(shifted, low_ref[at, :], high_ref[at, :])
+            cu = shifted - cz - state(at)[1]
+            if last:
+                mapped[iteration, 0, at, :] = cz
+                mapped[iteration, 1, at, :] = cu
+            else:
+                changes[iteration - 1, 0, at, :] = cz
+                changes[iteration - 1, 1, at, :] = cu
             sums[0] += column_sum(cz * mapped[0, 0, at, :] + cu * mapped[0, 1, at, :])
             for i in range(1, iteration):
                 sums[i] += column_sum(
@@ -347,10 +354,10 @@
 
         def keep(at):
             for j, before in enumerate(state(at)):
-                changes[iteration - 1, j, at, :] = mapped[iteration, j, at, :] - before
-
-        if not last:
-            chunks(local, size, keep)
+                change = mapped[iteration, j, at, :] if last else changes[iteration - 1, j, at, :]
+                mapped[iteration, j, at, :] = before + change
+
+        chunks(local, size, keep)
         for copy in reversed(spread):
             copy.wait_recv()
         whole = parts[0]
@@ -434,6 +441,8 @@
             pltpu.VMEM(big, jnp.float32),
             pltpu.VMEM((local // s, s), jnp.float32),
             pltpu.VMEM(big, jnp.float32),
+            pltpu.VMEM(big, jnp.float32),
+            pltpu.VMEM(big, jnp.float32),
             pltpu.VMEM(big, jnp.int32),
             pltpu.VMEM(big, jnp.int32),
             pltpu.VMEM(big, jnp.float32),
@@ -457,7 +466,7 @@
         ]
         + [dma] * 6,
         compiler_params=pltpu.CompilerParams(
-            collective_id=0, has_side_effects=True, vmem_limit_bytes=40 * 1024 * 1024
+            collective_id=0, has_side_effects=True, vmem_limit_bytes=42 * 1024 * 1024
         ),
         name="main",
     )(design_matrix, targets, linear, lines, lower_code, upper_code)

time: 66.4 us -> 65.7 us (0.989)
  Pallas kernels: 65.3 us -> 64.6 us
    pallas_call x1, Pallas kernels: 63.1 us -> 62.4 us  [per_device(): pl.pallas_call(functools.partial(main_kernel, n, size), in_specs=[hbm] *...]
where the time goes in v5:
time: 65.7 us; the launch traced here: 65.4 us
  Pallas kernels  64.6 us (98%)
  between operations  0.8 us (1%)
    pallas_call x1, Pallas kernels, per_device(): pl.pallas_call(functools.partial(main_kernel, n, size), in_specs=[hbm] *...  62.4 us
    pallas_call x1, Pallas kernels, per_device(): pl.pallas_call(functools.partial(mix_kernel, min(512, local)), in_specs=[...  2.24 us

profile of v5, /device:TPU:0, one launch (start us, length us, event | category | flops | bytes accessed | tf_op | source)
XLA Modules:
  0.0 65.4 jit_solution(11227702495830612167)
XLA Ops:
  0.6 62.4 %main.1 = (f32[4,2,4096,128]{3,2,1,0:T(8,128)S(1)}, f32[8,128]{1,0:T(8,128)S(1)}, f32[4096,128]{1,0:T(8,128)S(1)}, f32[4096,128]{1,0:T(8,128)S(1)}) custom-call(bf16[512,4096]{1,0:T(8,128)(2,1)} %a_hbm.1, f32[32,128]{1,0:T(8,128)} %targets_hbm.1, f32[4096,128]{1,0:T(8,128)} %lin_hbm.1, f32[32,128]{1,0:T(8,128)} %bitcast.1, s32[4096,128]{1,0:T(8,128)} %lo_hbm.1, ...), custom_call_target="tpu_custom_call" | custom-call | tf_op jit(solution)/shard_map/main/pallas_call | solution.py:427
  63.0 2.2 %last_mix.1 = (f32[4096,128]{1,0:T(8,128)}, f32[4096,128]{1,0:T(8,128)}) custom-call(f32[4,2,4096,128]{3,2,1,0:T(8,128)S(1)} %get-tuple-element.6.mapped, f32[8,128]{1,0:T(8,128)S(1)} %get-tuple-element.7.alpha_ref, f32[4096,128]{1,0:T(8,128)S(1)} %get-tuple-element.8.lower, f32[4096,128]{1,0:T(8,128)S(1)} %get-tuple-element.9.upper), custom_call_target="tpu_custom_call" | custom-call | tf_op jit(solution)/shard_map/last_mix/pallas_call | solution.py:473
